TPU v7x, 8 devices: a whole 2x2x1 slice. The times are simulated.
8 devices in a mesh: tp: 4 (over z, y, x), dp: 2 (over core).
Axes of the slice: x: 2, y: 2, z: 1, core: 2. Of those that a mesh axis runs over, the one named last changes fastest.
Arguments:
- x: bfloat16 [8, 2048, 1536], P('dp')
- lengths: int32 [8], P('dp')
- targets: int32 [8], P('dp')
- norm1: bfloat16 [2, 1536], replicated
- norm2: bfloat16 [2, 1536], replicated
- norm_f: bfloat16 [1536], replicated
- w_q: bfloat16 [2, 1536, 12, 128], P(None, ('dp', 'tp'))
- w_k: bfloat16 [2, 1536, 2, 128], P(None, ('dp', 'tp'))
- w_v: bfloat16 [2, 1536, 2, 128], P(None, ('dp', 'tp'))
- w_o: bfloat16 [2, 1536, 1536], P(None, ('dp', 'tp'))
- w_gate: bfloat16 [2, 1536, 8960], P(None, ('dp', 'tp'))
- w_up: bfloat16 [2, 1536, 8960], P(None, ('dp', 'tp'))
- w_down: bfloat16 [2, 8960, 1536], P(None, ('dp', 'tp'))
- w_lm: bfloat16 [1536, 151936], P(('dp', 'tp'))
Outputs:
- output 1: bfloat16 [2, 1536, 12, 128], P(None, None, 'tp')
- output 2: bfloat16 [2, 1536, 4, 128], P(None, None, 'tp')
- output 3: bfloat16 [2, 1536, 4, 128], P(None, None, 'tp')
- output 4: bfloat16 [2, 1536, 1536], P(None, 'tp')
- output 5: bfloat16 [2, 1536, 8960], P(None, None, 'tp')
- output 6: bfloat16 [2, 1536, 8960], P(None, None, 'tp')
- output 7: bfloat16 [2, 8960, 1536], P(None, 'tp')
- output 8: bfloat16 [2, 8, 4, 2048, 128], P(None, 'dp', 'tp')
- output 9: bfloat16 [2, 8, 4, 2048, 128], P(None, 'dp', 'tp')
- output 10: float32 [8], P('dp')
All inputs are finite; a program needn't handle non-finite values.
Results may differ from a plain program's by a relative error of at most 0.0107616.
Values are sent between devices in bfloat16 or wider.
A program may use at most 1 GiB of HBM per device.

v0:
```python
import jax
import jax.numpy as jnp
from jax import lax
from jax.sharding import PartitionSpec as P

ROPE_BASE = 10000.0
NORM_EPS = 1e-6


def rms_scale(hidden, gain):
    hidden32 = hidden.astype(jnp.float32)
    inv_rms = lax.rsqrt(jnp.mean(hidden32 * hidden32, axis=-1, keepdims=True) + NORM_EPS)
    return (hidden32 * inv_rms * gain.astype(jnp.float32)).astype(jnp.bfloat16)


def rope_tables(seq_len, head_dim):
    positions = jnp.arange(seq_len, dtype=jnp.float32)
    inv_freq = ROPE_BASE ** (-2.0 * jnp.arange(head_dim // 2, dtype=jnp.float32) / head_dim)
    angles = positions[:, None] * inv_freq[None, :]
    return jnp.cos(angles), jnp.sin(angles)


def apply_rope(projected, cos_tab, sin_tab):
    half_dim = projected.shape[-1] // 2
    lower_half = projected[..., :half_dim]
    upper_half = projected[..., half_dim:]
    cos_rows = cos_tab[:, None, :]
    sin_rows = sin_tab[:, None, :]
    return jnp.concatenate([lower_half * cos_rows - upper_half * sin_rows, upper_half * cos_rows + lower_half * sin_rows], axis=-1)


def residual_add(hidden, update):
    return (hidden.astype(jnp.float32) + update.astype(jnp.float32)).astype(jnp.bfloat16)


def solution(mesh):
    tp_size = mesh.shape['tp']
    dp_size = mesh.shape['dp']
    row_moves = [(tp_idx * dp_size + dp_idx, dp_idx * tp_size + tp_idx) for tp_idx in range(tp_size) for dp_idx in range(dp_size)]

    def to_columns(local_rows):
        row_count, col_count = local_rows.shape[0], local_rows.shape[1]
        trailing = tuple(local_rows.shape[2:])
        pieces = jnp.moveaxis(local_rows.reshape((row_count, tp_size, col_count // tp_size) + trailing), 1, 0)
        swapped = lax.all_to_all(pieces, 'tp', 0, 0)
        merged = swapped.reshape((tp_size * row_count, col_count // tp_size) + trailing)
        return lax.all_gather(merged, 'dp', axis=0, tiled=True)

    def to_rows(local_rows):
        moved = lax.ppermute(local_rows, ('tp', 'dp'), row_moves)
        return lax.all_gather(moved, 'dp', axis=0, tiled=True)

    def device_program(x, lengths, targets, norm1, norm2, norm_f, w_q, w_k, w_v, w_o, w_gate, w_up, w_down, w_lm):
        q_heads, head_dim = w_q.shape[2], w_q.shape[3]
        replicas = tp_size // w_k.shape[2]
        seq_len, model_dim = x.shape[1], x.shape[2]
        local_heads = q_heads // tp_size
        score_scale = head_dim ** -0.5
        cos_tab, sin_tab = rope_tables(seq_len, head_dim)
        positions = jnp.arange(seq_len)
        causal = positions[None, :] <= positions[:, None]
        visible = (causal[None] & (positions[None, None, :] < lengths[:, None, None]))[:, None]
        hidden = x
        q_rolls = []
        k_rolls = []
        v_rolls = []
        o_rolls = []
        gate_rolls = []
        up_rolls = []
        down_rolls = []
        k_caches = []
        v_caches = []
        for layer in range(w_q.shape[0]):
            wq_roll = to_columns(w_q[layer])
            wk_roll = to_columns(jnp.repeat(w_k[layer], replicas, axis=1))
            wv_roll = to_columns(jnp.repeat(w_v[layer], replicas, axis=1))
            wo_roll = to_rows(w_o[layer])
            wg_roll = to_columns(w_gate[layer])
            wu_roll = to_columns(w_up[layer])
            wd_roll = to_rows(w_down[layer])
            normed = rms_scale(hidden, norm1[layer])
            q_rot = apply_rope(jnp.einsum('bsd,dhe->bshe', normed, wq_roll, preferred_element_type=jnp.float32), cos_tab, sin_tab).astype(jnp.bfloat16)
            k_rot = apply_rope(jnp.einsum('bsd,dhe->bshe', normed, wk_roll, preferred_element_type=jnp.float32), cos_tab, sin_tab).astype(jnp.bfloat16)
            v_proj = jnp.einsum('bsd,dhe->bshe', normed, wv_roll, preferred_element_type=jnp.float32).astype(jnp.bfloat16)
            scores = jnp.einsum('bshe,bte->bhst', q_rot, k_rot[:, :, 0], preferred_element_type=jnp.float32) * score_scale
            scores = jnp.where(visible, scores, -1e30)
            attn_probs = jax.nn.softmax(scores, axis=-1).astype(jnp.bfloat16)
            attn_mix = jnp.einsum('bhst,bte->bshe', attn_probs, v_proj[:, :, 0], preferred_element_type=jnp.float32).astype(jnp.bfloat16)
            attn_part = jnp.einsum('bshe,hef->bsf', attn_mix, wo_roll.reshape(local_heads, head_dim, model_dim), preferred_element_type=jnp.float32)
            attn_out = lax.psum(attn_part.astype(jnp.bfloat16), 'tp')
            hidden = residual_add(hidden, attn_out)
            normed = rms_scale(hidden, norm2[layer])
            gate_proj = jnp.einsum('bsd,df->bsf', normed, wg_roll, preferred_element_type=jnp.float32)
            up_proj = jnp.einsum('bsd,df->bsf', normed, wu_roll, preferred_element_type=jnp.float32)
            activated = (jax.nn.silu(gate_proj) * up_proj).astype(jnp.bfloat16)
            down_part = jnp.einsum('bsf,fd->bsd', activated, wd_roll, preferred_element_type=jnp.float32)
            down_sum = lax.psum(down_part.astype(jnp.bfloat16), 'tp')
            hidden = residual_add(hidden, down_sum)
            q_rolls.append(wq_roll)
            k_rolls.append(wk_roll)
            v_rolls.append(wv_roll)
            o_rolls.append(wo_roll)
            gate_rolls.append(wg_roll)
            up_rolls.append(wu_roll)
            down_rolls.append(wd_roll)
            k_caches.append(jnp.swapaxes(k_rot, 1, 2))
            v_caches.append(jnp.swapaxes(v_proj, 1, 2))
        wlm_roll = to_columns(w_lm)
        pick = (positions[None, :] == lengths[:, None] - 1).astype(jnp.bfloat16)
        last_row = jnp.einsum('bs,bsd->bd', pick, hidden, preferred_element_type=jnp.float32).astype(jnp.bfloat16)
        logits = jnp.dot(rms_scale(last_row, norm_f), wlm_roll, preferred_element_type=jnp.float32)
        vocab_local = logits.shape[1]
        row_max = lax.pmax(jnp.max(logits, axis=1), 'tp')
        sum_exp = lax.psum(jnp.sum(jnp.exp(logits - row_max[:, None]), axis=1), 'tp')
        vocab_ids = lax.axis_index('tp') * vocab_local + jnp.arange(vocab_local)
        target_logit = lax.psum(jnp.sum(jnp.where(vocab_ids[None, :] == targets[:, None], logits, 0.0), axis=1), 'tp')
        logprob = target_logit - row_max - jnp.log(sum_exp)
        return (jnp.stack(q_rolls), jnp.stack(k_rolls), jnp.stack(v_rolls), jnp.stack(o_rolls), jnp.stack(gate_rolls), jnp.stack(up_rolls), jnp.stack(down_rolls), jnp.stack(k_caches), jnp.stack(v_caches), logprob)

    row_split = P(None, ('dp', 'tp'), None)
    head_rows = P(None, ('dp', 'tp'), None, None)
    head_cols = P(None, None, 'tp', None)
    col_split = P(None, None, 'tp')
    row_tp = P(None, 'tp', None)
    cache_spec = P(None, 'dp', 'tp', None, None)
    in_specs = (P('dp', None, None), P('dp'), P('dp'), P(), P(), P(), head_rows, head_rows, head_rows, row_split, row_split, row_split, row_split, P(('dp', 'tp'), None))
    out_specs = (head_cols, head_cols, head_cols, row_tp, col_split, col_split, row_tp, cache_spec, cache_spec, P('dp'))
    return jax.shard_map(device_program, mesh=mesh, in_specs=in_specs, out_specs=out_specs, check_vma=False)
```

profile of v0, /device:TPU:0, one launch (start us, length us, event | category | flops | bytes accessed | tf_op | source)
XLA Modules:
  0.0 3911.9 jit_solution(1692826883771613893)
XLA Ops:
  120.0 86.6 %fusion.125 = (f32[4,3,2048]{2,1,0:T(4,128)S(1)}, f32[4,3,2048,2048]{2,3,1,0:T(8,128)}) fusion(pred[4,2048,2048]{1,2,0:T(8,128)(4,1)} %broadcast_and_fusion, bf16[4,2048,3,64]{1,3,2,0:T(8,128)(2,1)} %get-tuple-element.77, bf16[4,2048,3,64]{1,3,2,0:T(8,128)(2,1)} %get-tuple-element.76, bf16[4,2048,64]{1,2,0:T(8,128)(2,1)S(1)} %bitcast.273, ...), kind=kOutput, calls=%fused_computation.169 | convolution fusion | flops 13103007744 | bytes 226590720 | tf_op jit(solution)/shard_map/sub | solution.py:87
  206.6 63.9 %fusion.148 = bf16[4,2048,3,128]{1,3,2,0:T(8,128)(2,1)} fusion(f32[4,3,2048,2048]{2,3,1,0:T(8,128)} %get-tuple-element.99, f32[4,3,2048]{2,1,0:T(4,128)S(1)} %get-tuple-element.98, bf16[4,2048,128]{2,1,0:T(8,128)(2,1)} %fusion.78), kind=kOutput, calls=%fused_computation.80.clone | convolution fusion | flops 12988710912 | bytes 209813504 | tf_op jit(solution)/shard_map/bhst,bte->bshe/dot_general | solution.py:88
  303.9 83.3 %all_to_all.55 = bf16[4,192,2240]{2,1,0:T(8,128)(2,1)S(1)} all-to-all(bf16[4,192,2240]{2,1,0:T(8,128)(2,1)S(1)} %bitcast.253), channel_id=1, replica_groups=mesh['tp'=4,'dp'=2] {'tp'}, dimensions={0} | all-to-all | bytes 6881280 | tf_op jit(solution)/shard_map/all_to_all | solution.py:45
  403.7 82.0 %all_to_all.56 = bf16[4,192,2240]{2,1,0:T(8,128)(2,1)S(1)} all-to-all(bf16[4,192,2240]{2,1,0:T(8,128)(2,1)S(1)} %bitcast.254), channel_id=1, replica_groups=mesh['tp'=4,'dp'=2] {'tp'}, dimensions={0} | all-to-all | bytes 6881280 | tf_op jit(solution)/shard_map/all_to_all | solution.py:45
  498.2 369.2 %all-reduce.6.cloned.1.call-done = bf16[4,2048,1536]{2,1,0:T(8,128)(2,1)} async-done(((bf16[4,2048,1536]{2,1,0:T(8,128)(2,1)}), bf16[4,2048,1536]{2,1,0:T(8,128)(2,1)}) %all-reduce.6.cloned.1.call-update) | async-done | bytes 25165840 | tf_op jit(solution)/shard_map/psum | solution.py:90
  867.5 28.9 fusion.16
  896.4 68.3 %fusion.41 = f32[4,2048,2240]{1,2,0:T(8,128)} fusion(bf16[4,2048,1536]{2,1,0:T(8,128)(2,1)} %get-tuple-element.73, f32[1536]{0:T(1024)S(1)} %get-tuple-element.63, f32[4,2048]{1,0:T(4,128)S(1)} %add_rsqrt_fusion.2, bf16[1536,2240]{0,1:T(8,128)(2,1)} %all-gather.24.cloned.1.call-done), kind=kOutput, calls=%fused_computation.62 | convolution fusion | flops 56421777408 | bytes 105486336 | tf_op jit(solution)/shard_map/bsd,df->bsf/dot_general | solution.py:94
  964.7 80.3 %multiply_convert_fusion.1.clone.2 = bf16[4,2048,2240]{1,2,0:T(8,128)(2,1)} fusion(f32[4,2048,2240]{1,2,0:T(8,128)} %fusion.41, bf16[4,2048,1536]{2,1,0:T(8,128)(2,1)} %get-tuple-element.73, f32[1536]{0:T(1024)S(1)} %get-tuple-element.63, f32[4,2048]{1,0:T(4,128)S(1)} %add_rsqrt_fusion.2, bf16[1536,2240]{0,1:T(8,128)(2,1)} %all-gather.20.cloned.1.call-done), kind=kOutput, calls=%fused_computation.31.clone.clone.clone | convolution fusion | flops 56531877888 | bytes 142186496 | tf_op jit(solution)/shard_map/bsd,df->bsf/dot_general | solution.py:93
  1045.0 66.7 %convolution_convert_fusion.1 = bf16[4,2048,1536]{2,1,0:T(8,128)(2,1)} fusion(bf16[2240,1536]{1,0:T(8,128)(2,1)} %all-gather.28.cloned.1.call-done, bf16[4,2048,2240]{1,2,0:T(8,128)(2,1)} %multiply_convert_fusion.1.clone.2), kind=kOutput, calls=%fused_computation.53 | convolution fusion | flops 56384028672 | bytes 68747264 | tf_op jit(solution)/shard_map/bsf,fd->bsd/dot_general | solution.py:96
  1182.3 385.7 %all-reduce.8.cloned.1.call-done = bf16[4,2048,1536]{2,1,0:T(8,128)(2,1)} async-done(((bf16[4,2048,1536]{2,1,0:T(8,128)(2,1)}), bf16[4,2048,1536]{2,1,0:T(8,128)(2,1)}) %all-reduce.8.cloned.1.call-update) | async-done | bytes 25165840 | tf_op jit(solution)/shard_map/psum | solution.py:97
  1647.0 86.6 %fusion.126 = (f32[4,3,2048]{2,1,0:T(4,128)S(1)}, f32[4,3,2048,2048]{2,3,1,0:T(8,128)}) fusion(pred[4,2048,2048]{1,2,0:T(8,128)(4,1)} %broadcast_and_fusion, bf16[4,2048,3,64]{1,3,2,0:T(8,128)(2,1)} %get-tuple-element.75, bf16[4,2048,3,64]{1,3,2,0:T(8,128)(2,1)} %get-tuple-element.74, bf16[4,2048,64]{1,2,0:T(8,128)(2,1)S(1)} %bitcast.277, ...), kind=kOutput, calls=%fused_computation.170 | convolution fusion | flops 13103007744 | bytes 226590720 | tf_op jit(solution)/shard_map/sub | solution.py:87
  1733.6 63.7 %fusion.145 = bf16[4,2048,3,128]{1,3,2,0:T(8,128)(2,1)} fusion(f32[4,3,2048,2048]{2,3,1,0:T(8,128)} %get-tuple-element.101, f32[4,3,2048]{2,1,0:T(4,128)S(1)} %get-tuple-element.100, bf16[4,2048,128]{2,1,0:T(8,128)(2,1)} %fusion.81), kind=kOutput, calls=%fused_computation.79.clone.1 | convolution fusion | flops 12988710912 | bytes 209813504 | tf_op jit(solution)/shard_map/bhst,bte->bshe/dot_general | solution.py:88
  1824.5 82.7 %all_to_all.58 = bf16[4,192,2240]{2,1,0:T(8,128)(2,1)S(1)} all-to-all(bf16[4,192,2240]{2,1,0:T(8,128)(2,1)S(1)} %bitcast.255), channel_id=1, replica_groups=mesh['tp'=4,'dp'=2] {'tp'}, dimensions={0} | all-to-all | bytes 6881280 | tf_op jit(solution)/shard_map/all_to_all | solution.py:45
  1917.3 81.5 %all_to_all.59 = bf16[4,192,2240]{2,1,0:T(8,128)(2,1)S(1)} all-to-all(bf16[4,192,2240]{2,1,0:T(8,128)(2,1)S(1)} %bitcast.256), channel_id=1, replica_groups=mesh['tp'=4,'dp'=2] {'tp'}, dimensions={0} | all-to-all | bytes 6881280 | tf_op jit(solution)/shard_map/all_to_all | solution.py:45
  2005.0 56.2 %reshape.338 = bf16[192,4,37984]{2,1,0:T(4,128)(2,1)} reshape(bf16[192,151936]{1,0:T(8,128)(2,1)} %param.27) | data formatting | bytes 116686848 | tf_op jit(solution)/shard_map/reshape | solution.py:44
  2061.2 39.9 %copy.204 = bf16[192,4,37984]{2,0,1:T(8,128)(2,1)} copy(bf16[192,4,37984]{2,1,0:T(4,128)(2,1)} %reshape.338) | data formatting | bytes 116686848 | tf_op jit(solution)/shard_map/reshape | solution.py:44
  2115.7 894.9 %all-reduce.10.cloned.1.call-done = bf16[4,2048,1536]{2,1,0:T(8,128)(2,1)} async-done(((bf16[4,2048,1536]{2,1,0:T(8,128)(2,1)}), bf16[4,2048,1536]{2,1,0:T(8,128)(2,1)}) %all-reduce.10.cloned.1.call-update) | async-done | bytes 25165840 | tf_op jit(solution)/shard_map/psum | solution.py:90
  3039.6 68.3 %fusion.38 = f32[4,2048,2240]{1,2,0:T(8,128)} fusion(bf16[4,2048,1536]{2,1,0:T(8,128)(2,1)} %get-tuple-element.69, f32[1536]{0:T(1024)S(1)} %copy-done.35, f32[4,2048]{1,0:T(4,128)S(1)} %add_rsqrt_fusion, bf16[1536,2240]{0,1:T(8,128)(2,1)} %all-gather.26.cloned.1.call-done), kind=kOutput, calls=%fused_computation.61 | convolution fusion | flops 56421777408 | bytes 105486336 | tf_op jit(solution)/shard_map/bsd,df->bsf/dot_general | solution.py:94
  3107.9 80.4 %multiply_convert_fusion.clone.4 = bf16[4,2048,2240]{1,2,0:T(8,128)(2,1)} fusion(f32[4,2048,2240]{1,2,0:T(8,128)} %fusion.38, bf16[4,2048,1536]{2,1,0:T(8,128)(2,1)} %get-tuple-element.69, f32[1536]{0:T(1024)S(1)} %copy-done.35, f32[4,2048]{1,0:T(4,128)S(1)} %add_rsqrt_fusion, bf16[1536,2240]{0,1:T(8,128)(2,1)} %all-gather.22.cloned.1.call-done), kind=kOutput, calls=%fused_computation.30.clone.clone.clone.1 | convolution fusion | flops 56531877888 | bytes 142186496 | tf_op jit(solution)/shard_map/bsd,df->bsf/dot_general | solution.py:93
  3188.3 67.1 %convolution_convert_fusion = bf16[4,2048,1536]{2,1,0:T(8,128)(2,1)} fusion(bf16[2240,1536]{1,0:T(8,128)(2,1)} %all-gather.30.cloned.1.call-done, bf16[4,2048,2240]{1,2,0:T(8,128)(2,1)} %multiply_convert_fusion.clone.4), kind=kOutput, calls=%fused_computation.52 | convolution fusion | flops 56384028672 | bytes 68747264 | tf_op jit(solution)/shard_map/bsf,fd->bsd/dot_general | solution.py:96
  3315.2 373.4 %all-reduce.12.cloned.1.call-done = bf16[4,2048,1536]{2,1,0:T(8,128)(2,1)} async-done(((bf16[4,2048,1536]{2,1,0:T(8,128)(2,1)}), bf16[4,2048,1536]{2,1,0:T(8,128)(2,1)}) %all-reduce.12.cloned.1.call-update) | async-done | bytes 25165840 | tf_op jit(solution)/shard_map/psum | solution.py:97
  3688.6 29.2 fusion.28
  3717.9 129.8 %all-gather.32.cloned.1.call-done = bf16[1536,37984]{1,0:T(8,128)(2,1)} async-done(((bf16[768,37984]{1,0:T(8,128)(2,1)}), bf16[1536,37984]{1,0:T(8,128)(2,1)}) %all-gather.32.cloned.1.call-update) | async-done | bytes 116686864 | tf_op jit(solution)/shard_map/all_gather | solution.py:47
  3847.8 38.1 fusion.127
  (236 shorter events, 490.2 us)
Async XLA Ops:
  9.6 41.4 %all-to-all-start.4 = ((bf16[4,192,1,128]{3,1,2,0:T(8,128)(2,1)}), bf16[4,192,1,128]{3,1,2,0:T(8,128)(2,1)S(1)}, u32[]{:S(2)}, u32[]{:S(2)}) async-start(bf16[4,192,1,128]{3,1,2,0:T(8,128)(2,1)} %bitcast.20), calls=%async_computation.4 | async-start | bytes 393216 | tf_op jit(solution)/shard_map/all_to_all | solution.py:45
  17.5 76.3 %collective-permute-start = (bf16[192,1536]{1,0:T(8,128)(2,1)}, bf16[192,1536]{1,0:T(8,128)(2,1)}, u32[]{:S(2)}, u32[]{:S(2)}) collective-permute-start(bf16[192,1536]{1,0:T(8,128)(2,1)} %get-tuple-element.88), channel_id=1, source_target_pairs={{0,0},{1,4},{2,1},{3,5},{4,2},{5,6},{6,3},{7,7}} | collective-permute-start | bytes 1769480 | tf_op jit(solution)/shard_map/ppermute | solution.py:50
  51.7 8.5 all-to-all-start.2
  60.3 18.7 all-to-all-start
  63.8 30.1 all-gather.12.cloned.1.call-start
  80.1 190.4 %all-gather.16.cloned.1.call-start = ((), (), s32[]{:S(2)}) async-start(), calls=%async_computation.13 | async-start | bytes 1769472 | tf_op jit(solution)/shard_map/all_gather | solution.py:51
  93.8 773.6 %all-reduce.6.cloned.1.call-start = ((), (), s32[]{:S(2)}) async-start(), calls=%async_computation.21 | async-start | bytes 50331648 | tf_op jit(solution)/shard_map/psum | solution.py:90
  290.8 605.6 %all-gather.24.cloned.1.call-start = ((), (), s32[]{:S(2)}) async-start(), calls=%async_computation.17 | async-start | bytes 10321920 | tf_op jit(solution)/shard_map/all_gather | solution.py:47
  390.7 574.0 %all-gather.20.cloned.1.call-start = ((), (), s32[]{:S(2)}) async-start(), calls=%async_computation.15 | async-start | bytes 10321920 | tf_op jit(solution)/shard_map/all_gather | solution.py:47
  489.2 555.8 %all-gather.28.cloned.1.call-start = ((), (), s32[]{:S(2)}) async-start(), calls=%async_computation.19 | async-start | bytes 10321920 | tf_op jit(solution)/shard_map/all_gather | solution.py:51
  498.2 1069.9 %all-reduce.8.cloned.1.call-start = ((), (), s32[]{:S(2)}) async-start(), calls=%async_computation.22 | async-start | bytes 50331648 | tf_op jit(solution)/shard_map/psum | solution.py:97
  1111.8 483.0 %all-gather.14.cloned.1.call-start = ((), (), s32[]{:S(2)}) async-start(), calls=%async_computation.12 | async-start | bytes 1769472 | tf_op jit(solution)/shard_map/all_gather | solution.py:47
  1133.6 47.7 %collective-permute-start.1 = (bf16[192,1536]{1,0:T(8,128)(2,1)S(1)}, bf16[192,1536]{1,0:T(8,128)(2,1)S(1)}, u32[]{:S(2)}, u32[]{:S(2)}) collective-permute-start(bf16[192,1536]{1,0:T(8,128)(2,1)S(1)} %copy-done.28), channel_id=1, source_target_pairs={{0,0},{1,4},{2,1},{3,5},{4,2},{5,6},{6,3},{7,7}} | collective-permute-start | bytes 1769480 | tf_op jit(solution)/shard_map/ppermute | solution.py:50
  1135.1 32.3 all-to-all-start.3
  1168.1 11.2 all-to-all-start.5
  1172.0 625.4 %all-gather.18.cloned.1.call-start = ((), (), s32[]{:S(2)}) async-start(), calls=%async_computation.14 | async-start | bytes 1769472 | tf_op jit(solution)/shard_map/all_gather | solution.py:51
  1182.3 1828.4 %all-reduce.10.cloned.1.call-start = ((), (), s32[]{:S(2)}) async-start(), calls=%async_computation.23 | async-start | bytes 50331648 | tf_op jit(solution)/shard_map/psum | solution.py:90
  1817.9 1221.7 %all-gather.26.cloned.1.call-start = ((), (), s32[]{:S(2)}) async-start(), calls=%async_computation.18 | async-start | bytes 10321920 | tf_op jit(solution)/shard_map/all_gather | solution.py:47
  1910.7 1197.2 %all-gather.22.cloned.1.call-start = ((), (), s32[]{:S(2)}) async-start(), calls=%async_computation.16 | async-start | bytes 10321920 | tf_op jit(solution)/shard_map/all_gather | solution.py:47
  2002.3 111.5 %collective-permute-start.3 = (bf16[1120,1536]{1,0:T(8,128)(2,1)}, bf16[1120,1536]{1,0:T(8,128)(2,1)S(1)}, u32[]{:S(2)}, u32[]{:S(2)}) collective-permute-start(bf16[1120,1536]{1,0:T(8,128)(2,1)} %get-tuple-element.79), channel_id=1, source_target_pairs={{0,0},{1,4},{2,1},{3,5},{4,2},{5,6},{6,3},{7,7}} | collective-permute-start | bytes 10321928 | tf_op jit(solution)/shard_map/ppermute | solution.py:50
  2101.1 1154.4 %all-to-all-start.10 = ((bf16[4,192,37984]{2,1,0:T(8,128)(2,1)}), bf16[4,192,37984]{2,1,0:T(8,128)(2,1)}, u32[]{:S(2)}, u32[]{:S(2)}) async-start(bf16[4,192,37984]{2,1,0:T(8,128)(2,1)} %bitcast.252), calls=%async_computation.10 | async-start | bytes 116785152 | tf_op jit(solution)/shard_map/all_to_all | solution.py:45
  2113.8 1074.5 %all-gather.30.cloned.1.call-start = ((), (), s32[]{:S(2)}) async-start(), calls=%async_computation.20 | async-start | bytes 10321920 | tf_op jit(solution)/shard_map/all_gather | solution.py:51
  2115.7 1572.9 %all-reduce.12.cloned.1.call-start = ((), (), s32[]{:S(2)}) async-start(), calls=%async_computation.24 | async-start | bytes 50331648 | tf_op jit(solution)/shard_map/psum | solution.py:97
  3255.4 592.4 %all-gather.32.cloned.1.call-start = ((), (), s32[]{:S(2)}) async-start(), calls=%async_computation.25 | async-start | bytes 175177728 | tf_op jit(solution)/shard_map/all_gather | solution.py:47
  (45 other events, 3177.4 us)
Sparse Core Ops, SparseCore 0:
  80.2 7.7 all-gather.11
  93.9 7.7 all-gather.15
  290.9 576.4 all-reduce.5
  869.4 15.5 all-gather.23
  886.9 16.0 all-gather.19
  904.3 16.0 all-gather.27
  1111.9 456.1 all-reduce.7
  1570.1 7.1 all-gather.13
  1579.4 7.6 all-gather.17
  1818.0 1192.5 all-reduce.9
  3012.7 15.5 all-gather.25
  3030.2 16.0 all-gather.21
  3048.4 16.0 all-gather.29
  3255.5 433.0 all-reduce.11
  3689.9 157.7 all-gather.31
where the time goes:
time: 3920 us; the launch traced here: 3910 us
  waiting for transfers between devices  2190 us (56%)
  matrix products  929 us (24%)
  blocking collectives  376 us (10%)
  local copies, waits for them, and re-layouts  183 us (5%)
  other arithmetic  177 us (5%)
  starting transfers between devices  45 us (1%)
    psum x2, waiting for transfers between devices, device_program(): attn_out = lax.psum(attn_part.astype(jnp.bfloat16), 'tp')  1260 us
    psum x2, waiting for transfers between devices, device_program(): down_sum = lax.psum(down_part.astype(jnp.bfloat16), 'tp')  759 us
    all_to_all x5, blocking collectives, to_columns(): swapped = lax.all_to_all(pieces, 'tp', 0, 0)  349 us
    sub x2, matrix products, device_program(): attn_probs = jax.nn.softmax(scores, axis=-1).astype(jnp.bfloat16)  173 us
    dot_general x2, matrix products, device_program(): jnp.einsum('bsd,df->bsf', normed, wg_roll, preferred_element_type=jnp.flo...  161 us
    dot_general x2, matrix products, device_program(): jnp.einsum('bsd,df->bsf', normed, wu_roll, preferred_element_type=jnp.flo...  137 us
    dot_general x2, matrix products, device_program(): jnp.einsum('bsf,fd->bsd', activated, wd_roll, preferred_element_type=jnp....  134 us
    all_gather x7, waiting for transfers between devices, to_columns(): return lax.all_gather(merged, 'dp', axis=0, tiled=True)  130 us
  transfers between devices with their start and end apart: 25, of which 8 were waited for; matrix products, arithmetic and copies ran while one was open for 29% of the time, Pallas kernels for 0%

commit v1 on v0

v1 whole, which is shorter than its diff:
```python
import functools
import math

import jax
import jax.numpy as jnp
from jax import lax
from jax.experimental import pallas as pl
from jax.experimental.pallas import tpu as pltpu
from jax.sharding import PartitionSpec as P


ROPE_BASE = 10000.0
NORM_EPS = 1e-6
F32 = jnp.float32
BF16 = jnp.bfloat16


def rms_scale(hidden, gain):
    hidden32 = hidden.astype(F32)
    inv_rms = lax.rsqrt(jnp.mean(hidden32 * hidden32, axis=-1, keepdims=True) + NORM_EPS)
    return (hidden32 * inv_rms * gain.astype(F32)).astype(BF16)


def rope_tables(positions, head_dim):
    inv_freq = ROPE_BASE ** (-2.0 * jnp.arange(head_dim // 2, dtype=F32) / head_dim)
    angles = positions.astype(F32)[:, None] * inv_freq[None, :]
    return jnp.cos(angles), jnp.sin(angles)


def residual_add(hidden, update):
    return (hidden.astype(F32) + update.astype(F32)).astype(BF16)


def dot32(a, b):
    return jnp.dot(a, b, preferred_element_type=F32)


def roped_kernel(n_rope, head_dim, idx_ref, x_ref, gain_ref, w_ref, cos_ref, sin_ref, o_ref):
    x32 = x_ref[0].astype(F32)
    inv_rms = lax.rsqrt(jnp.mean(x32 * x32, axis=-1, keepdims=True) + NORM_EPS)
    z = (x32 * inv_rms * gain_ref[...]).astype(BF16)
    width = w_ref.shape[1]
    chunk = 2 * head_dim if width % (2 * head_dim) == 0 else head_dim
    for start in range(0, width, chunk):
        p = dot32(z, w_ref[:, start:start + chunk])
        for off in range(0, chunk, head_dim):
            piece = p[:, off:off + head_dim]
            if (start + off) // head_dim < n_rope:
                piece = piece * cos_ref[...] + pltpu.roll(piece, head_dim // 2, 1) * sin_ref[...]
            o_ref[:, start + off:start + off + head_dim] = piece.astype(BF16)


def norm_proj_rope(x, which, n_seq, gain, w, col_block, width, n_rope, cos_full, sin_full):
    _, seq_len, model_dim = x.shape
    head_dim = cos_full.shape[1]
    bm = 256
    per = seq_len // bm
    return pl.pallas_call(
        functools.partial(roped_kernel, n_rope, head_dim),
        grid_spec=pltpu.PrefetchScalarGridSpec(
            num_scalar_prefetch=1,
            grid=(n_seq * per,),
            in_specs=[
                pl.BlockSpec((1, bm, model_dim), lambda i, s: (s[0] + i // per, i % per, 0)),
                pl.BlockSpec((1, model_dim), lambda i, s: (0, 0)),
                pl.BlockSpec((model_dim, width), lambda i, s: (0, col_block)),
                pl.BlockSpec((bm, head_dim), lambda i, s: (i % per, 0)),
                pl.BlockSpec((bm, head_dim), lambda i, s: (i % per, 0)),
            ],
            out_specs=pl.BlockSpec((bm, width), lambda i, s: (i, 0)),
        ),
        out_shape=jax.ShapeDtypeStruct((n_seq * seq_len, width), BF16),
        compiler_params=pltpu.CompilerParams(dimension_semantics=("arbitrary",)),
        cost_estimate=pl.CostEstimate(flops=2 * n_seq * seq_len * model_dim * width, bytes_accessed=2 * n_seq * seq_len * (model_dim + width), transcendentals=0),
        name="norm_proj_rope",
    )(which, x, gain.astype(F32)[None], w, cos_full, sin_full)


def out_proj_kernel(idx_ref, mix_ref, w_ref, x_ref, gain_ref, h_ref, z_ref):
    update = dot32(mix_ref[...], w_ref[...]).astype(BF16)
    hidden = residual_add(x_ref[0], update)
    h_ref[...] = hidden
    z_ref[...] = rms_scale(hidden, gain_ref[...])


def out_proj_norm(x, which, mix, w, gain):
    _, seq_len, model_dim = x.shape
    bm = 256
    row = jax.ShapeDtypeStruct((seq_len, model_dim), BF16)
    return pl.pallas_call(
        out_proj_kernel,
        grid_spec=pltpu.PrefetchScalarGridSpec(
            num_scalar_prefetch=1,
            grid=(seq_len // bm,),
            in_specs=[
                pl.BlockSpec((bm, mix.shape[1]), lambda i, s: (i, 0)),
                pl.BlockSpec(w.shape, lambda i, s: (0, 0)),
                pl.BlockSpec((1, bm, model_dim), lambda i, s: (s[0], i, 0)),
                pl.BlockSpec((1, model_dim), lambda i, s: (0, 0)),
            ],
            out_specs=[pl.BlockSpec((bm, model_dim), lambda i, s: (i, 0))] * 2,
        ),
        out_shape=[row, row],
        compiler_params=pltpu.CompilerParams(dimension_semantics=("arbitrary",)),
        cost_estimate=pl.CostEstimate(flops=2 * seq_len * model_dim * model_dim, bytes_accessed=8 * seq_len * model_dim, transcendentals=0),
        name="out_proj_norm",
    )(which, mix, w, x, gain.astype(F32)[None])


def block_t_kernel(win, cols, bm, off_ref, w_ref, *rest):
    o_ref, buf, sem = rest[-3:]
    i = pl.program_id(0)

    def fetch(j):
        src = w_ref.at[pl.ds(j * bm, bm), pl.ds(pl.multiple_of(off_ref[0], 128), win)]
        return pltpu.make_async_copy(src, buf.at[j % 2], sem.at[j % 2])

    @pl.when(i == 0)
    def _():
        fetch(i).start()

    @pl.when(i + 1 < pl.num_programs(0))
    def _():
        fetch(i + 1).start()

    fetch(i).wait()
    flipped = buf[i % 2].T
    o_ref[0] = jnp.where(off_ref[1] == 1, flipped[win - cols:, :], flipped[:cols, :])


def block_transposed(w, layer, n_layers, off, cols, prev):
    rows = w.shape[0]
    bm, win = 128, (cols + 127) // 128 * 128
    off = jnp.stack([off // 128 * 128, jnp.where(off % 128 != 0, 1, 0)]).astype(jnp.int32)
    extra = () if prev is None else (prev,)
    return pl.pallas_call(
        functools.partial(block_t_kernel, win, cols, bm),
        grid_spec=pltpu.PrefetchScalarGridSpec(
            num_scalar_prefetch=1,
            grid=(rows // bm,),
            in_specs=[pl.BlockSpec(memory_space=pl.ANY)] * (1 + len(extra)),
            out_specs=pl.BlockSpec((1, cols, bm), lambda i, s: (layer, 0, i)),
            scratch_shapes=[pltpu.VMEM((2, bm, win), BF16), pltpu.SemaphoreType.DMA((2,))],
        ),
        out_shape=jax.ShapeDtypeStruct((n_layers, cols, rows), BF16),
        input_output_aliases={} if prev is None else {2: 0},
        compiler_params=pltpu.CompilerParams(dimension_semantics=("arbitrary",)),
        cost_estimate=pl.CostEstimate(flops=20 * rows * win * 128, bytes_accessed=4 * rows * cols, transcendentals=0),
        name="block_transposed",
    )(off, w, *extra)


def pieces_t_kernel(col, win, cols, rows, n_pieces, idx_ref, *refs):
    pieces, (o_ref, buf, sem) = refs[:n_pieces], refs[-3:]
    i = pl.program_id(0)

    def fetch(j, run):
        for k, ref in enumerate(pieces):
            @pl.when(j == k // 2)
            def _():
                half = (k % 2) ^ idx_ref[0]
                copy = pltpu.make_async_copy(ref.at[:, pl.ds(col, win)], buf.at[j % 2, pl.ds(half * rows, rows)], sem.at[j % 2, k % 2])
                copy.start() if run else copy.wait()

    @pl.when(i == 0)
    def _():
        fetch(i, True)

    @pl.when(i + 1 < pl.num_programs(0))
    def _():
        fetch(i + 1, True)

    fetch(i, False)
    o_ref[0] = buf[i % 2].T[:cols, :]


def pieces_transposed(pieces, layer, tp, dp, tp_size, col, cols, prev):
    rows = pieces[0].shape[0]
    n_pieces = len(pieces)
    win = (cols + 127) // 128 * 128
    idx = jnp.stack([tp % 2, tp // 2, dp]).astype(jnp.int32)
    per = tp_size // 2

    def where(i, s):
        return (layer, 0, (s[2] ^ (i // per)) * per + (s[1] ^ (i % per)))

    return pl.pallas_call(
        functools.partial(pieces_t_kernel, col, win, cols, rows, n_pieces),
        grid_spec=pltpu.PrefetchScalarGridSpec(
            num_scalar_prefetch=1,
            grid=(n_pieces // 2,),
            in_specs=[pl.BlockSpec(memory_space=pl.ANY)] * (n_pieces + 1),
            out_specs=pl.BlockSpec((1, cols, 2 * rows), where),
            scratch_shapes=[pltpu.VMEM((2, 2 * rows, win), BF16), pltpu.SemaphoreType.DMA((2, 2))],
        ),
        out_shape=jax.ShapeDtypeStruct(prev.shape, BF16),
        input_output_aliases={n_pieces + 1: 0},
        compiler_params=pltpu.CompilerParams(dimension_semantics=("arbitrary",)),
        cost_estimate=pl.CostEstimate(flops=20 * rows * 8 * win * 128, bytes_accessed=32 * rows * cols, transcendentals=0),
        name="pieces_transposed",
    )(idx, *pieces, prev)


def pieces_rows_kernel(idx_ref, *refs):
    i = pl.program_id(0)
    for k, ref in enumerate(refs[:-1]):
        @pl.when(i == k)
        def _():
            refs[-1][...] = ref[...]


def pieces_rows(pieces, me, cols):
    rows, n_pieces = pieces[0].shape[0], len(pieces)
    return pl.pallas_call(
        pieces_rows_kernel,
        grid_spec=pltpu.PrefetchScalarGridSpec(
            num_scalar_prefetch=1,
            grid=(n_pieces,),
            in_specs=[pl.BlockSpec((rows, cols), lambda i, s: (0, 0))] * n_pieces,
            out_specs=pl.BlockSpec((rows, cols), lambda i, s: (s[0] ^ i, 0)),
        ),
        out_shape=jax.ShapeDtypeStruct((n_pieces * rows, cols), BF16),
        compiler_params=pltpu.CompilerParams(dimension_semantics=("arbitrary",)),
        cost_estimate=pl.CostEstimate(flops=0, bytes_accessed=4 * n_pieces * rows * cols, transcendentals=0),
        name="pieces_rows",
    )(me[None].astype(jnp.int32), *pieces)


def last_rows_kernel(tp_size, dp_size, q_heads, kv_heads, head_dim, len_ref, row_ref, kv_ref, wq_ref, wo_ref, wg_ref, wu_ref, wd_ref, n1_ref, n2_ref, nf_ref, cos_ref, sin_ref, u_ref,
                     g_st, g_rv, a_st, a_rv, s_st, s_rv, f_st, f_rv, q_s, mix_s, rows_s, act_s, send_sem, recv_sem):
    tp, dp = lax.axis_index('tp'), lax.axis_index('dp')
    n_dev = tp_size * dp_size
    shard, ffn_shard = wq_ref.shape[0], wd_ref.shape[0]

    def peer(k):
        return tp ^ (k % tp_size), dp ^ (k // tp_size)

    def slot(k):
        t, d = peer(k)
        return d * tp_size + t

    barrier = pltpu.get_barrier_semaphore()
    for k in range(1, n_dev):
        pl.semaphore_signal(barrier, inc=1, device_id=peer(k), device_id_type=pl.DeviceIdType.MESH)
    pl.semaphore_wait(barrier, n_dev - 1)

    def exchange(step, src, dst):
        copies = [pltpu.make_async_remote_copy(
            src_ref=src(k), dst_ref=dst.at[k], send_sem=send_sem.at[step, k], recv_sem=recv_sem.at[step, k],
            device_id=peer(k), device_id_type=pl.DeviceIdType.MESH) for k in range(1, n_dev)]
        for c in copies:
            c.start()
        for c in copies:
            c.wait()

    def gather(step, value, stage, landed, rows_ref, width):
        for i in range(n_dev):
            stage[i, :, :width] = value[:, i * width:(i + 1) * width]
        exchange(step, lambda k: stage.at[slot(k)], landed)
        rows_ref[0:1, :] = stage[slot(0)]
        for k in range(1, n_dev):
            rows_ref[k:k + 1, :] = landed[k]
        return rows_ref[:, :width].astype(BF16)

    def scatter(step, parts, stage, landed):
        at = 0
        for p in parts:
            for k in range(1, n_dev):
                stage[k, :, at:at + p.shape[1]] = p[k:k + 1, :]
            at += p.shape[1]
        exchange(step, lambda k: stage.at[k], landed)
        out, at = [], 0
        for p in parts:
            total = p[0:1, :]
            for k in range(1, n_dev):
                total = total + landed[k, :, at:at + p.shape[1]]
            out.append(total)
            at += p.shape[1]
        return out

    def norm(hidden, gain_ref):
        return rms_scale(hidden, gain_ref[...]).astype(F32)

    for ref in (g_st, a_st):
        ref[...] = jnp.zeros_like(ref)
    hidden = row_ref[...]
    z = gather(0, norm(hidden, n1_ref), g_st.at[0], g_rv.at[0], rows_s, shard)
    q_row, = scatter(1, [dot32(z, wq_ref[...])], s_st.at[0], s_rv.at[0])
    group = q_heads // kv_heads
    q_s[...] = jnp.zeros_like(q_s)
    for h in range(q_heads):
        piece = q_row[:, h * head_dim:(h + 1) * head_dim]
        at = h // group * 8 + h % group
        q_s[at:at + 1, :] = piece * cos_ref[...] + pltpu.roll(piece, head_dim // 2, 1) * sin_ref[...]
    seq_len = kv_ref.shape[0]
    seen = lax.broadcasted_iota(jnp.int32, (8, seq_len), 1) < len_ref[0]
    for g in range(kv_heads):
        keys = kv_ref[:, g * head_dim:(g + 1) * head_dim]
        values = kv_ref[:, (kv_heads + g) * head_dim:(kv_heads + g + 1) * head_dim]
        scores = lax.dot_general(q_s[g * 8:g * 8 + 8, :].astype(BF16), keys, (((1,), (1,)), ((), ())), preferred_element_type=F32) * head_dim ** -0.5
        scores = jnp.where(seen, scores, -1e30)
        e = jnp.exp(scores - jnp.max(scores, axis=1, keepdims=True))
        probs = (e / jnp.sum(e, axis=1, keepdims=True)).astype(BF16)
        mix = dot32(probs, values).astype(BF16).astype(F32)
        for j in range(group):
            h = g * group + j
            mix_s[:, h * head_dim:(h + 1) * head_dim] = mix[j:j + 1, :]
    z = gather(2, mix_s[...], g_st.at[1], g_rv.at[1], rows_s, shard)
    update, = scatter(3, [dot32(z, wo_ref[...])], s_st.at[1], s_rv.at[1])
    hidden = residual_add(hidden, update.astype(BF16))
    z = gather(4, norm(hidden, n2_ref), g_st.at[2], g_rv.at[2], rows_s, shard)
    gate, up = scatter(5, [dot32(z, wg_ref[...]), dot32(z, wu_ref[...])], f_st, f_rv)
    act = (gate / (1.0 + jnp.exp(-gate)) * up).astype(BF16).astype(F32)
    a = gather(6, act, a_st, a_rv, act_s, ffn_shard)
    update, = scatter(7, [dot32(a, wd_ref[...])], s_st.at[2], s_rv.at[2])
    hidden = residual_add(hidden, update.astype(BF16))
    u_ref[...] = gather(8, norm(hidden, nf_ref), g_st.at[3], g_rv.at[3], rows_s, shard)


def last_rows(mesh, length, row, kv, wq, wo, wg, wu, wd, gains, cos_row, sin_row, q_heads, kv_heads):
    tp_size, dp_size = mesh.shape['tp'], mesh.shape['dp']
    n_dev = tp_size * dp_size
    shard, model_dim = wo.shape
    ffn, ffn_shard = wg.shape[1], wd.shape[0]
    head_dim = cos_row.shape[1]
    pad = lambda n: (n + 127) // 128 * 128
    buf = lambda *lead: pltpu.VMEM(lead[:-1] + (n_dev, 1, lead[-1]), F32)
    vmem = pl.BlockSpec(memory_space=pltpu.VMEM)
    return pl.pallas_call(
        functools.partial(last_rows_kernel, tp_size, dp_size, q_heads, kv_heads, head_dim),
        in_specs=[pl.BlockSpec(memory_space=pltpu.SMEM)] + [vmem] * 12,
        out_specs=vmem,
        out_shape=jax.ShapeDtypeStruct((n_dev, shard), BF16),
        scratch_shapes=[
            buf(4, pad(shard)), buf(4, pad(shard)),
            buf(pad(ffn_shard)), buf(pad(ffn_shard)),
            buf(3, model_dim), buf(3, model_dim),
            buf(2 * ffn), buf(2 * ffn),
            pltpu.VMEM((8 * kv_heads, head_dim), F32),
            pltpu.VMEM((1, q_heads * head_dim), F32),
            pltpu.VMEM((n_dev, pad(shard)), F32),
            pltpu.VMEM((n_dev, pad(ffn_shard)), F32),
            pltpu.SemaphoreType.DMA((9, n_dev)),
            pltpu.SemaphoreType.DMA((9, n_dev)),
        ],
        compiler_params=pltpu.CompilerParams(collective_id=0, has_side_effects=True),
        cost_estimate=pl.CostEstimate(flops=20 * 10**9, bytes_accessed=2 * (wq.size + wo.size + wg.size + wu.size + wd.size), transcendentals=0),
        name="last_rows",
    )(length, row, kv, wq, wo, wg, wu, wd, *gains, cos_row, sin_row)


def split_kernel(starts, widths, *refs):
    o_ref = refs[-1]
    o_ref[...] = jnp.zeros_like(o_ref)
    for ref, start, width in zip(refs[:-1], starts, widths):
        for s in range(o_ref.shape[0]):
            o_ref[s, :, start:start + width] = ref[0, :, s * width:(s + 1) * width]


def split_columns(arrays, n_parts, starts, total):
    rows = arrays[0].shape[1]
    bm = 48
    widths = [a.shape[2] // n_parts for a in arrays]
    last = lambda n: (lambda i: (n - 1, i, 0))
    return pl.pallas_call(
        functools.partial(split_kernel, starts, widths),
        grid=(rows // bm,),
        in_specs=[pl.BlockSpec((1, bm, a.shape[2]), last(a.shape[0])) for a in arrays],
        out_specs=pl.BlockSpec((n_parts, bm, total), lambda i: (0, i, 0)),
        out_shape=jax.ShapeDtypeStruct((n_parts, rows, total), BF16),
        cost_estimate=pl.CostEstimate(flops=20 * rows * total * 128, bytes_accessed=4 * rows * total * n_parts, transcendentals=0),
        name="split_columns",
    )(*arrays)


def attn_kernel(block_rows, head_dim, n_blocks, n_pack, len_ref, q_ref, k_ref, v_ref, o_ref):
    step = pl.program_id(1)
    length = len_ref[0]
    factor = head_dim ** -0.5 * math.log2(math.e)
    trans = (((1,), (1,)), ((), ()))
    for blk in range(n_blocks):
        @pl.when(step == blk)
        def _(blk=blk):
            base = blk * block_rows
            shape = (block_rows, block_rows)
            rows = lax.broadcasted_iota(jnp.int32, shape, 0) + base
            cols = lax.broadcasted_iota(jnp.int32, shape, 1) + base
            diag_ok = cols <= jnp.minimum(rows, length - 1)
            if base:
                past_ok = lax.broadcasted_iota(jnp.int32, (1, base), 1) < length
                past_bias = jnp.where(past_ok, 0.0, -1e30)
            for h in range(n_pack):
                q = q_ref[:, h * head_dim:(h + 1) * head_dim]
                s_diag = lax.dot_general(q, k_ref[base:base + block_rows, :], trans, preferred_element_type=F32)
                s_diag = jnp.where(diag_ok, s_diag, -1e30)
                top = jnp.max(s_diag, axis=1, keepdims=True)
                if base:
                    s_past = lax.dot_general(q, k_ref[:base, :], trans, preferred_element_type=F32) + past_bias
                    top = jnp.maximum(top, jnp.max(s_past, axis=1, keepdims=True))
                shift = top * factor
                e_diag = jnp.exp2(s_diag * factor - shift)
                total = jnp.sum(e_diag, axis=1, keepdims=True)
                if base:
                    e_past = jnp.exp2(s_past * factor - shift)
                    total = total + jnp.sum(e_past, axis=1, keepdims=True)
                inv = 1.0 / total
                mix = dot32((e_diag * inv).astype(BF16), v_ref[base:base + block_rows, :])
                if base:
                    mix = mix + dot32((e_past * inv).astype(BF16), v_ref[:base, :])
                o_ref[:, h * head_dim:(h + 1) * head_dim] = mix.astype(BF16)


def attention(qkv, length, q_heads, kv_heads, head_dim):
    seq_len = qkv.shape[0]
    block_rows = 256
    n_blocks = seq_len // block_rows
    n_pack = 2
    group = q_heads // kv_heads // n_pack
    kern = functools.partial(attn_kernel, block_rows, head_dim, n_blocks, n_pack)
    return pl.pallas_call(
        kern,
        grid=(q_heads // n_pack, n_blocks),
        in_specs=[
            pl.BlockSpec(memory_space=pltpu.SMEM),
            pl.BlockSpec((block_rows, n_pack * head_dim), lambda h, i: (i, h)),
            pl.BlockSpec((seq_len, head_dim), lambda h, i: (0, q_heads + h // group)),
            pl.BlockSpec((seq_len, head_dim), lambda h, i: (0, q_heads + kv_heads + h // group)),
        ],
        out_specs=pl.BlockSpec((block_rows, n_pack * head_dim), lambda h, i: (i, h)),
        out_shape=jax.ShapeDtypeStruct((seq_len, q_heads * head_dim), BF16),
        compiler_params=pltpu.CompilerParams(dimension_semantics=("arbitrary", "arbitrary")),
        cost_estimate=pl.CostEstimate(flops=2 * seq_len * seq_len * q_heads * head_dim * 2, bytes_accessed=4 * seq_len * q_heads * head_dim, transcendentals=seq_len * seq_len * q_heads // 2),
        name="causal_attention",
    )(length, qkv, qkv, qkv)


def solution(mesh):
    tp_size = mesh.shape['tp']
    dp_size = mesh.shape['dp']
    both_axes = ('dp', 'tp')
    both_names = ('tp', 'dp')
    direct_moves, relay_first, relay_second, relay_ends = [], [], [], []
    for t in range(tp_size):
        for d in range(dp_size):
            to_t, to_d = divmod(d * tp_size + t, dp_size)
            if t ^ to_t == tp_size - 1:
                mid = (to_t & 2) | (t & 1)
                relay_first.append((t * dp_size + d, mid * dp_size + d))
                relay_second.append((mid * dp_size + d, to_t * dp_size + to_d))
                relay_ends.append((to_t, to_d))
            else:
                direct_moves.append((t * dp_size + d, to_t * dp_size + to_d))
    swap_cores = [(0, 1), (1, 0)]

    def xor_moves(bit):
        return [(i, i ^ bit) for i in range(tp_size)]

    def gather_all(rows):
        return lax.all_gather(rows, both_axes, axis=0, tiled=True)

    def whole_program(x, lengths, targets, norm1, norm2, norm_f, w_q, w_k, w_v, w_o, w_gate, w_up, w_down, w_lm):
        tp = lax.axis_index('tp')
        dp = lax.axis_index('dp')
        me = dp * tp_size + tp
        q_heads, head_dim = w_q.shape[2], w_q.shape[3]
        kv_heads = w_k.shape[2]
        replicas = tp_size // kv_heads
        n_seq, seq_len, model_dim = x.shape
        loc_heads = q_heads // tp_size
        q_width, kv_width, loc_q = q_heads * head_dim, kv_heads * head_dim, loc_heads * head_dim
        shard = w_q.shape[1]
        ffn = w_gate.shape[2]
        ffn_loc = ffn // tp_size
        my_kv = tp // replicas
        cos_tab, sin_tab = rope_tables(jnp.arange(seq_len), head_dim)
        cos_full = jnp.concatenate([cos_tab, cos_tab], axis=1)
        sin_full = jnp.concatenate([-sin_tab, sin_tab], axis=1)
        mine = tp[None].astype(jnp.int32)
        first = jnp.zeros((1,), jnp.int32)

        flat = lambda w: w.reshape(shard, -1)
        n_layers = w_q.shape[0]
        attn_rows = jnp.concatenate([flat(w_q[0]), flat(w_k[0]), flat(w_v[0]), w_o[0], flat(w_k[1]), flat(w_v[1])], axis=1)
        attn_full = gather_all(attn_rows)
        wg0 = gather_all(w_gate[0])
        wu0 = gather_all(w_up[0])
        cut = model_dim * 2 // 3
        wd0a = gather_all(w_down[0][:, :cut])
        wd0b = gather_all(w_down[0][:, cut:])
        qkv_width = q_width + 2 * kv_width
        kv1_at = qkv_width + q_width
        wo0 = attn_full[:, qkv_width:kv1_at]

        my_head = lambda at: lax.dynamic_slice_in_dim(attn_full, at + my_kv * head_dim, head_dim, 1)
        wk0, wv0 = my_head(q_width), my_head(q_width + kv_width)
        wk1, wv1 = my_head(kv1_at), my_head(kv1_at + kv_width)
        qkv = norm_proj_rope(x, mine, 1, norm1[0], attn_full, 0, qkv_width, q_heads + kv_heads, cos_full, sin_full)
        length = lax.dynamic_index_in_dim(lengths, tp, 0)
        mix = attention(qkv, length, q_heads, kv_heads, head_dim)
        hidden, z = out_proj_norm(x, mine, mix, wo0, norm2[0])
        gate = dot32(z, wg0)
        wkv0 = jnp.concatenate([wk0, wv0], axis=1)
        kv_mine = norm_proj_rope(x, first, n_seq, norm1[0], wkv0, 0, 2 * head_dim, 1, cos_full, sin_full)
        kv_mine = kv_mine.reshape(n_seq, seq_len, 2 * head_dim)
        act = (jax.nn.silu(gate) * dot32(z, wu0)).astype(BF16)
        gate_t = block_transposed(wg0, 0, n_layers, tp * ffn_loc, ffn_loc, None)
        hidden_a = residual_add(hidden[:, :cut], dot32(act, wd0a).astype(BF16))
        up_t = block_transposed(wu0, 0, n_layers, tp * ffn_loc, ffn_loc, None)

        pad = lambda n: (n + 127) // 128 * 128
        starts = [0, pad(loc_q), pad(loc_q) + pad(ffn_loc)]
        total = starts[2] + pad(ffn_loc)
        by_target = split_columns([flat(w_q[1])[None], w_gate, w_up], tp_size, starts, total)
        wo_rows, wd_rows = w_o[1], w_down[1]
        pieces = []
        for bit in range(tp_size):
            piece = lax.dynamic_index_in_dim(by_target, tp ^ bit, 0, keepdims=False)
            if bit:
                piece = lax.ppermute(piece, 'tp', xor_moves(bit))
            pieces.append(piece)

        def to_rows(local_rows):
            moved = lax.ppermute(local_rows, both_names, direct_moves)
            relay = lax.ppermute(local_rows, both_names, relay_first)
            return moved, relay

        wo1, wo_relay = to_rows(wo_rows)
        wd1, wd_relay = to_rows(wd_rows)
        hidden_b = residual_add(hidden[:, cut:], dot32(act, wd0b).astype(BF16))
        hidden = jnp.concatenate([hidden_a, hidden_b], axis=1)

        kv1 = norm_proj_rope(hidden[None], first, 1, norm1[1], attn_full, kv1_at // (2 * kv_width), 2 * kv_width, kv_heads, cos_full, sin_full)
        k1 = lambda i: lax.dynamic_slice_in_dim(kv1, i * head_dim, head_dim, 1)
        v1 = lambda i: lax.dynamic_slice_in_dim(kv1, kv_width + i * head_dim, head_dim, 1)
        k_cache1 = jnp.zeros((n_seq, seq_len, head_dim), BF16)
        v_cache1 = jnp.zeros((n_seq, seq_len, head_dim), BF16)
        for bit in range(tp_size):
            head = (tp ^ bit) // replicas
            piece = jnp.stack([k1(head), v1(head)])
            if bit:
                piece = lax.ppermute(piece, 'tp', xor_moves(bit))
            k_cache1 = lax.dynamic_update_slice(k_cache1, piece[:1], (tp ^ bit, 0, 0))
            v_cache1 = lax.dynamic_update_slice(v_cache1, piece[1:], (tp ^ bit, 0, 0))

        row = lax.dynamic_slice_in_dim(hidden, length[0] - 1, 1, 0)
        cos_r, sin_r = rope_tables(length - 1, head_dim)
        gains = [g.astype(F32)[None] for g in (norm1[1], norm2[1], norm_f)]
        u = last_rows(mesh, length, row, kv1, flat(w_q[1]), w_o[1], w_gate[1], w_up[1], w_down[1], gains,
                      jnp.concatenate([cos_r, cos_r], axis=1), jnp.concatenate([-sin_r, sin_r], axis=1), q_heads, kv_heads)

        part = dot32(u, w_lm)
        part = part[:n_seq] + lax.ppermute(part[n_seq:], 'dp', swap_cores)
        logits = part[:1]
        for bit in range(1, tp_size):
            logits = logits + lax.ppermute(part[bit:bit + 1], 'tp', xor_moves(bit))
        top = jnp.max(logits, axis=1, keepdims=True)
        lse = top + jnp.log(jnp.sum(jnp.exp(logits - top), axis=1, keepdims=True))
        target = lax.dynamic_index_in_dim(targets, tp, 0, keepdims=False)
        hit = jnp.arange(logits.shape[1])[None, :] == target
        logprob = jnp.sum(jnp.where(hit, logits, 0.0), axis=1) - lse[:, 0]
        logprob = lax.all_gather(logprob, 'tp', axis=0, tiled=True)

        relayed = functools.reduce(jnp.logical_or, [jnp.logical_and(tp == t, dp == d) for t, d in relay_ends])
        wo1 = jnp.where(relayed, lax.ppermute(wo_relay, both_names, relay_second), wo1)
        wd1 = jnp.where(relayed, lax.ppermute(wd_relay, both_names, relay_second), wd1)
        pieces = pieces + [lax.ppermute(p, 'dp', swap_cores) for p in pieces]
        wo1b = lax.ppermute(wo1, 'dp', swap_cores)
        wd1b = lax.ppermute(wd1, 'dp', swap_cores)
        heads = lambda w: w.reshape(model_dim, -1, head_dim)

        def pair(a, b):
            out = jnp.zeros((2,) + a.shape, BF16)
            return lax.dynamic_update_slice(lax.dynamic_update_slice(out, a[None], (dp, 0, 0)), b[None], (1 - dp, 0, 0)).reshape(2 * a.shape[0], a.shape[1])

        wq1 = pieces_rows(pieces, me, loc_q)
        q_out = jnp.stack([heads(lax.dynamic_slice_in_dim(attn_full, tp * loc_q, loc_q, 1)), heads(wq1)])
        k_out = jnp.stack([heads(wk0), heads(wk1)])
        v_out = jnp.stack([heads(wv0), heads(wv1)])
        o_out = jnp.stack([lax.dynamic_slice_in_dim(wo0, tp * loc_q, loc_q, 0), pair(wo1, wo1b)])
        gate_t = pieces_transposed(pieces, 1, tp, dp, tp_size, starts[1], ffn_loc, gate_t)
        up_t = pieces_transposed(pieces, 1, tp, dp, tp_size, starts[2], ffn_loc, up_t)
        gate_out = jnp.swapaxes(gate_t, 1, 2)
        up_out = jnp.swapaxes(up_t, 1, 2)
        rows_of = lambda w: lax.dynamic_slice_in_dim(w, tp * ffn_loc, ffn_loc, 0)
        down_out = jnp.stack([jnp.concatenate([rows_of(wd0a), rows_of(wd0b)], axis=1), pair(wd1, wd1b)])
        k_cache = jnp.stack([kv_mine[:, :, :head_dim], k_cache1])[:, :, None]
        v_cache = jnp.stack([kv_mine[:, :, head_dim:], v_cache1])[:, :, None]
        return (q_out, k_out, v_out, o_out, gate_out, up_out, down_out, k_cache, v_cache, logprob)

    row_split = P(None, ('dp', 'tp'), None)
    head_rows = P(None, ('dp', 'tp'), None, None)
    head_cols = P(None, None, 'tp', None)
    col_split = P(None, None, 'tp')
    row_tp = P(None, 'tp', None)
    cache_spec = P(None, 'dp', 'tp', None, None)
    in_specs = (P('dp', None, None), P('dp'), P('dp'), P(), P(), P(), head_rows, head_rows, head_rows, row_split, row_split, row_split, row_split, P(('dp', 'tp'), None))
    out_specs = (head_cols, head_cols, head_cols, row_tp, col_split, col_split, row_tp, cache_spec, cache_spec, P('dp'))
    return jax.shard_map(whole_program, mesh=mesh, in_specs=in_specs, out_specs=out_specs, check_vma=False)
```

time: 3920 us -> 1010 us (0.26)
  waiting for transfers between devices: 2190 us -> 273 us
  matrix products: 929 us -> 237 us
  blocking collectives: 376 us -> 9.36 us
  Pallas kernels: 0 us -> 262 us
  other arithmetic: 177 us -> 64.1 us
  local copies, waits for them, and re-layouts: 183 us -> 95.1 us
    psum x4 -> x0, waiting for transfers between devices: 2020 us -> none  [the longest x2 1260 us: device_program(): attn_out = lax.psum(attn_part.astype(jnp.bfloat16), 'tp')]
    dot_general x18 -> x5, matrix products: 755 us -> 237 us  [dot32(): return jnp.dot(a, b, preferred_element_type=F32)]
    all_to_all x5 -> x0, blocking collectives: 349 us -> none  [to_columns(): swapped = lax.all_to_all(pieces, 'tp', 0, 0)]
    ppermute x4 -> x22, waiting for transfers between devices: 0.01 us -> 273 us  [the longest x1 95.2 us: whole_program(): lax.ppermute(wd_relay, both_names, relay_second)]
    pallas_call x0 -> x12, Pallas kernels: none -> 262 us  [the longest x1 83.3 us: attention(): pl.pallas_call(kern, grid=(q_heads // n_pack, n_blocks), in_specs=[pl.Blo...]
    sub x2 -> x0, matrix products: 173 us -> none  [device_program(): attn_probs = jax.nn.softmax(scores, axis=-1).astype(jnp.bfloat16)]
    all_gather x11 -> x5, waiting for transfers between devices: 130 us -> 0.03 us  [gather_all(): return lax.all_gather(rows, both_axes, axis=0, tiled=True)]
    reshape x10 -> x0, local copies, waits for them, and re-layouts: 113 us -> none  [the longest x2 96.1 us: to_columns(): local_rows.reshape((row_count, tp_size, col_count // tp_size) + trailing)]
  transfers between devices with their start and end apart: 25 -> 27, of which waited for: 8 -> 7; matrix products, arithmetic and copies ran while one was open for 29% -> 20% of each run, Pallas kernels for 0% -> 20%
where the time goes in v1:
time: 1010 us
  waiting for transfers between devices  273 us (27%)
  Pallas kernels  262 us (26%)
  matrix products  237 us (23%)
  local copies, waits for them, and re-layouts  95.1 us (9%)
  other arithmetic  64.1 us (6%)
  starting transfers between devices  47 us (5%)
  between operations  17.9 us (2%)
    dot_general x5, matrix products, dot32(): return jnp.dot(a, b, preferred_element_type=F32)  237 us
    ppermute x1, waiting for transfers between devices, whole_program(): lax.ppermute(wd_relay, both_names, relay_second)  95.2 us
    ppermute x1, waiting for transfers between devices, whole_program(): lax.ppermute(wo_relay, both_names, relay_second)  93.2 us
    pallas_call x1, Pallas kernels, attention(): pl.pallas_call(kern, grid=(q_heads // n_pack, n_blocks), in_specs=[pl.Blo...  83.3 us
    pallas_call x3, Pallas kernels, norm_proj_rope(): pl.pallas_call(functools.partial(roped_kernel, n_rope, head_dim), grid_sp...  65.2 us
    ppermute x2, waiting for transfers between devices, to_rows(): relay = lax.ppermute(local_rows, both_names, relay_first)  63.8 us
    pallas_call x1, Pallas kernels, last_rows(): pl.pallas_call(functools.partial(last_rows_kernel, tp_size, dp_size, q_he...  46.2 us
    ppermute x2, starting transfers between devices, to_rows(): moved = lax.ppermute(local_rows, both_names, direct_moves)  28.2 us
  transfers between devices with their start and end apart: 27, of which 7 were waited for; matrix products, arithmetic and copies ran while one was open for 20% of the time, Pallas kernels for 20%

profile of v1, /device:TPU:0, one launch (start us, length us, event | category | flops | bytes accessed | tf_op | source)
XLA Modules:
  0.0 1005.5 jit_solution(9110055601113434768)
XLA Ops:
  37.9 27.5 %collective-permute-start.13 = (bf16[1120,1536]{1,0:T(8,128)(2,1)}, bf16[1120,1536]{1,0:T(8,128)(2,1)}, u32[]{:S(2)}, u32[]{:S(2)}) collective-permute-start(bf16[1120,1536]{1,0:T(8,128)(2,1)} %get-tuple-element.45.wd_ref), channel_id=1, source_target_pairs={{0,0},{1,4},{2,1},{5,6},{6,3},{7,7}} | collective-permute-start | bytes 10321928 | tf_op jit(solution)/shard_map/ppermute | solution.py:523
  65.4 55.0 %collective-permute-done.11 = bf16[1120,1536]{1,0:T(8,128)(2,1)} collective-permute-done((bf16[1120,1536]{1,0:T(8,128)(2,1)}, bf16[1120,1536]{1,0:T(8,128)(2,1)}, u32[]{:S(2)}, u32[]{:S(2)}) %collective-permute-start.11) | collective-permute-done | bytes 3440672 | tf_op jit(solution)/shard_map/ppermute | solution.py:524
  139.6 8.8 collective-permute-done.7
  148.5 95.2 %collective-permute-done.12 = bf16[1120,1536]{1,0:T(8,128)(2,1)} collective-permute-done((bf16[1120,1536]{1,0:T(8,128)(2,1)}, bf16[1120,1536]{1,0:T(8,128)(2,1)}, u32[]{:S(2)}, u32[]{:S(2)}) %collective-permute-start.12) | collective-permute-done | bytes 3440672 | tf_op jit(solution)/shard_map/ppermute | solution.py:565
  258.4 93.2 %collective-permute-done.8 = bf16[192,1536]{1,0:T(8,128)(2,1)S(1)} collective-permute-done((bf16[192,1536]{1,0:T(8,128)(2,1)}, bf16[192,1536]{1,0:T(8,128)(2,1)S(1)}, u32[]{:S(2)}, u32[]{:S(2)}) %collective-permute-start.8) | collective-permute-done | bytes 589856 | tf_op jit(solution)/shard_map/ppermute | solution.py:564
  406.6 33.3 %norm_proj_rope.3 = bf16[8192,256]{1,0:T(8,128)(2,1)} custom-call(s32[1]{0:T(128)} %constant.171.clone.1.idx_ref, bf16[4,2048,1536]{2,1,0:T(8,128)(2,1)} %x_ref.5, f32[1,1536]{1,0:T(1,128)} %get-tuple-element.83.gain_ref, bf16[1536,256]{1,0:T(8,128)(2,1)} %pad_maximum_fusion.11.w_ref, f32[2048,128]{1,0:T(8,128)} %get-tuple-element.79.cos_ref, ...), custom_call_target="tpu_custom_call" | custom-call | flops 6442450944 | bytes 29360128 | tf_op jit(solution)/shard_map/norm_proj_rope/pallas_call | solution.py:58
  444.9 21.0 %norm_proj_rope.4.q_ref.k_ref.v_ref = bf16[2048,2048]{1,0:T(8,128)(2,1)} custom-call(s32[1]{0:T(128)} %bitcast.34.idx_ref, bf16[4,2048,1536]{2,1,0:T(8,128)(2,1)} %x_ref.5, f32[1,1536]{1,0:T(1,128)} %get-tuple-element.83.gain_ref, bf16[1536,4096]{1,0:T(8,128)(2,1)} %all-gather.8.cloned.1.call-done.w_ref, f32[2048,128]{1,0:T(8,128)} %get-tuple-element.79.cos_ref, ...), custom_call_target="tpu_custom_call" | custom-call | flops 12884901888 | bytes 14680064 | tf_op jit(solution)/shard_map/norm_proj_rope/pallas_call | solution.py:58
  465.8 83.3 %causal_attention.1.mix_ref = bf16[2048,1536]{1,0:T(8,128)(2,1)} custom-call(s32[1]{0:T(128)} %dynamic_slice.84.len_ref, bf16[2048,2048]{1,0:T(8,128)(2,1)} %norm_proj_rope.4.q_ref.k_ref.v_ref, bf16[2048,2048]{1,0:T(8,128)(2,1)} %norm_proj_rope.4.q_ref.k_ref.v_ref, bf16[2048,2048]{1,0:T(8,128)(2,1)} %norm_proj_rope.4.q_ref.k_ref.v_ref), custom_call_target="tpu_custom_call" | custom-call | flops 25769803776 | bytes 12582912 | tf_op jit(solution)/shard_map/causal_attention/pallas_call | solution.py:420
  549.1 17.8 %out_proj_norm.1 = (bf16[2048,1536]{1,0:T(8,128)(2,1)}, bf16[2048,1536]{1,0:T(8,128)(2,1)}) custom-call(s32[1]{0:T(128)} %bitcast.34.idx_ref, bf16[2048,1536]{1,0:T(8,128)(2,1)} %causal_attention.1.mix_ref, bf16[1536,1536]{1,0:T(8,128)(2,1)} %copy-done.1, bf16[4,2048,1536]{2,1,0:T(8,128)(2,1)} %x_ref.5, f32[1,1536]{1,0:T(1,128)} %get-tuple-element.74.gain_ref), custom_call_target="tpu_custom_call" | custom-call | flops 9663676416 | bytes 25165824 | tf_op jit(solution)/shard_map/out_proj_norm/pallas_call | solution.py:90
  574.9 12.6 %pad_maximum_fusion = bf16[2,2240,1536]{2,1,0:T(8,128)(2,1)} fusion(bf16[1,2240,1536]{2,1,0:T(8,128)(2,1)} %bitcast.31, bf16[1,2240,1536]{2,1,0:T(8,128)(2,1)} %maximum_bitcast_fusion), kind=kLoop, calls=%fused_computation.1 | loop fusion | flops 6881280 | bytes 27525120 | tf_op jit(solution)/shard_map/stack | solution.py:585
  587.4 66.9 %fusion.15 = f32[2048,8960]{1,0:T(8,128)} fusion(bf16[2048,1536]{1,0:T(8,128)(2,1)} %get-tuple-element.13, bf16[1,1536,8960]{2,1,0:T(8,128)(2,1)} %all-gather.14.cloned.1.call-done), kind=kOutput, calls=%fused_computation.100 | convolution fusion | flops 56371445760 | bytes 107216896 | tf_op jit(solution)/shard_map/dot_general | solution.py:35
  654.4 75.5 %multiply_convert_fusion = bf16[2048,8960]{1,0:T(8,128)(2,1)} fusion(f32[2048,8960]{1,0:T(8,128)} %fusion.15, bf16[2048,1536]{1,0:T(8,128)(2,1)} %get-tuple-element.13, bf16[1,1536,8960]{2,1,0:T(8,128)(2,1)} %all-gather.16.cloned.1.call-done), kind=kOutput, calls=%fused_computation | convolution fusion | flops 56481546240 | bytes 143917056 | tf_op jit(solution)/shard_map/dot_general | solution.py:35
  729.9 47.8 %add_convert_fusion = bf16[2048,1024]{1,0:T(8,128)(2,1)S(1)} fusion(bf16[2048,1536]{1,0:T(8,128)(2,1)} %get-tuple-element.12, bf16[2048,8960]{1,0:T(8,128)(2,1)} %multiply_convert_fusion, bf16[8960,1024]{1,0:T(8,128)(2,1)} %all-gather.10.cloned.1.call-done), kind=kOutput, calls=%fused_computation.2 | convolution fusion | flops 37591449600 | bytes 63438848 | tf_op jit(solution)/shard_map/dot_general | solution.py:35
  777.7 26.0 %add_convert_fusion.1 = bf16[2048,512]{1,0:T(8,128)(2,1)S(1)} fusion(bf16[2048,8960]{1,0:T(8,128)(2,1)} %multiply_convert_fusion, bf16[8960,512]{1,0:T(8,128)(2,1)} %all-gather.12.cloned.1.call-done, bf16[2048,1536]{1,0:T(8,128)(2,1)} %get-tuple-element.12), kind=kOutput, calls=%fused_computation.10 | convolution fusion | flops 18795724800 | bytes 50069504 | tf_op jit(solution)/shard_map/dot_general | solution.py:35
  807.6 10.9 %norm_proj_rope.5.kv_ref = bf16[2048,512]{1,0:T(8,128)(2,1)} custom-call(s32[1]{0:T(128)} %constant.171.clone.1.idx_ref, bf16[1,2048,1536]{2,1,0:T(8,128)(2,1)} %fusion.x_ref, f32[1,1536]{1,0:T(1,128)} %get-tuple-element.84.gain_ref.n1_ref, bf16[1536,4096]{1,0:T(8,128)(2,1)} %all-gather.8.cloned.1.call-done.w_ref, f32[2048,128]{1,0:T(8,128)} %get-tuple-element.79.cos_ref, ...), custom_call_target="tpu_custom_call" | custom-call | flops 3221225472 | bytes 8388608 | tf_op jit(solution)/shard_map/norm_proj_rope/pallas_call | solution.py:58
  818.4 46.2 %last_rows.1 = bf16[8,192]{1,0:T(8,128)(2,1)} custom-call(s32[1]{0:T(128)} %dynamic_slice.84.len_ref, bf16[1,1536]{1,0:T(2,128)(2,1)} %fusion.11.row_ref, bf16[2048,512]{1,0:T(8,128)(2,1)} %norm_proj_rope.5.kv_ref, bf16[192,1536]{1,0:T(8,128)(2,1)} %bitcast.165, bf16[192,1536]{1,0:T(8,128)(2,1)} %copy-done.15, bf16[192,8960]{1,0:T(8,128)(2,1)} %get-tuple-element.42.wg_ref, ...), custom_call_target="tpu_custom_call" | custom-call | flops 20000000000 | bytes 11501568 | tf_op jit(solution)/shard_map/last_rows/pallas_call | solution.py:329
  864.6 20.7 %fusion.24 = f32[8,151936]{1,0:T(8,128)S(1)} fusion(bf16[8,192]{1,0:T(8,128)(2,1)} %last_rows.1, bf16[192,151936]{1,0:T(8,128)(2,1)} %param.27), kind=kOutput, calls=%fused_computation.109 | convolution fusion | flops 466747392 | bytes 63208448 | tf_op jit(solution)/shard_map/dot_general | solution.py:35
  895.7 11.2 %block_transposed.3.refs_8_ = bf16[2,2240,1536]{2,1,0:T(8,128)(2,1)} custom-call(s32[2]{0:T(128)} %pad_add_fusion.1.off_ref, bf16[1536,8960]{1,0:T(8,128)(2,1)} %bitcast.155), custom_call_target="tpu_custom_call" | custom-call | flops 9059696640 | bytes 13762560 | tf_op jit(solution)/shard_map/block_transposed/pallas_call | solution.py:136
  906.9 11.2 %block_transposed.2.refs_8_ = bf16[2,2240,1536]{2,1,0:T(8,128)(2,1)} custom-call(s32[2]{0:T(128)} %pad_add_fusion.1.off_ref, bf16[1536,8960]{1,0:T(8,128)(2,1)} %bitcast.154), custom_call_target="tpu_custom_call" | custom-call | flops 9059696640 | bytes 13762560 | tf_op jit(solution)/shard_map/block_transposed/pallas_call | solution.py:136
  918.1 7.7 pieces_transposed.3
  930.8 7.7 pieces_transposed.2
  957.0 8.1 collective-permute-done.19
  965.1 12.0 %collective-permute-done.20 = f32[1,151936]{1,0:T(1,128)S(1)} collective-permute-done((f32[1,151936]{1,0:T(1,128)S(1)}, f32[1,151936]{1,0:T(1,128)S(1)}, u32[]{:S(2)}, u32[]{:S(2)}) %collective-permute-start.20) | collective-permute-done | bytes 607776 | tf_op jit(solution)/shard_map/ppermute | solution.py:555
  989.4 9.4 all-reduce
  (182 shorter events, 178.7 us)
Async XLA Ops:
  7.2 379.7 %all-gather.12.cloned.1.call-start = ((), (), s32[]{:S(2)}) async-start(), calls=%async_computation.2 | async-start | bytes 10321920 | tf_op jit(solution)/shard_map/all_gather | solution.py:459
  13.6 376.5 %all-gather.8.cloned.1.call-start = ((), (), s32[]{:S(2)}) async-start(), calls=%async_computation | async-start | bytes 14155776 | tf_op jit(solution)/shard_map/all_gather | solution.py:459
  21.8 545.1 %all-gather.10.cloned.1.call-start = ((), (), s32[]{:S(2)}) async-start(), calls=%async_computation.1 | async-start | bytes 20643840 | tf_op jit(solution)/shard_map/all_gather | solution.py:459
  23.7 563.8 %all-gather.14.cloned.1.call-start = ((), (), s32[]{:S(2)}) async-start(), calls=%async_computation.3 | async-start | bytes 30965760 | tf_op jit(solution)/shard_map/all_gather | solution.py:459
  30.1 624.3 %all-gather.16.cloned.1.call-start = ((), (), s32[]{:S(2)}) async-start(), calls=%async_computation.4 | async-start | bytes 30965760 | tf_op jit(solution)/shard_map/all_gather | solution.py:459
  36.5 83.9 %collective-permute-start.11 = (bf16[1120,1536]{1,0:T(8,128)(2,1)}, bf16[1120,1536]{1,0:T(8,128)(2,1)}, u32[]{:S(2)}, u32[]{:S(2)}) collective-permute-start(bf16[1120,1536]{1,0:T(8,128)(2,1)} %get-tuple-element.45.wd_ref), channel_id=1, source_target_pairs={{3,7},{4,0}} | collective-permute-start | bytes 10321928 | tf_op jit(solution)/shard_map/ppermute | solution.py:524
  37.9 110.6 %collective-permute-start.13 = (bf16[1120,1536]{1,0:T(8,128)(2,1)}, bf16[1120,1536]{1,0:T(8,128)(2,1)}, u32[]{:S(2)}, u32[]{:S(2)}) collective-permute-start(bf16[1120,1536]{1,0:T(8,128)(2,1)} %get-tuple-element.45.wd_ref), channel_id=1, source_target_pairs={{0,0},{1,4},{2,1},{5,6},{6,3},{7,7}} | collective-permute-start | bytes 10321928 | tf_op jit(solution)/shard_map/ppermute | solution.py:523
  120.4 123.3 %collective-permute-start.12 = (bf16[1120,1536]{1,0:T(8,128)(2,1)}, bf16[1120,1536]{1,0:T(8,128)(2,1)}, u32[]{:S(2)}, u32[]{:S(2)}) collective-permute-start(bf16[1120,1536]{1,0:T(8,128)(2,1)} %collective-permute-done.11), channel_id=1, source_target_pairs={{7,5},{0,2}} | collective-permute-start | bytes 10321928 | tf_op jit(solution)/shard_map/ppermute | solution.py:565
  123.5 25.0 %collective-permute-start.7 = (bf16[192,1536]{1,0:T(8,128)(2,1)S(1)}, bf16[192,1536]{1,0:T(8,128)(2,1)}, u32[]{:S(2)}, u32[]{:S(2)}) collective-permute-start(bf16[192,1536]{1,0:T(8,128)(2,1)S(1)} %slice_bitcast_fusion.6.wo_ref), channel_id=1, source_target_pairs={{3,7},{4,0}} | collective-permute-start | bytes 1769480 | tf_op jit(solution)/shard_map/ppermute | solution.py:524
  124.8 132.8 %collective-permute-start.9 = (bf16[192,1536]{1,0:T(8,128)(2,1)S(1)}, bf16[192,1536]{1,0:T(8,128)(2,1)S(1)}, u32[]{:S(2)}, u32[]{:S(2)}) collective-permute-start(bf16[192,1536]{1,0:T(8,128)(2,1)S(1)} %slice_bitcast_fusion.6.wo_ref), channel_id=1, source_target_pairs={{0,0},{1,4},{2,1},{5,6},{6,3},{7,7}} | collective-permute-start | bytes 1769480 | tf_op jit(solution)/shard_map/ppermute | solution.py:523
  139.6 223.2 %collective-permute-start = (bf16[192,4992]{1,0:T(8,128)(2,1)}, bf16[192,4992]{1,0:T(8,128)(2,1)}, u32[]{:S(2)}, u32[]{:S(2)}) collective-permute-start(bf16[192,4992]{1,0:T(8,128)(2,1)} %get-tuple-element.38), channel_id=1, source_target_pairs={{0,2},{2,0},{4,6},{6,4},{1,3},{3,1},{5,7},{7,5}} | collective-permute-start | bytes 5750792 | tf_op jit(solution)/shard_map/ppermute | solution.py:519
  148.5 214.5 %collective-permute-start.1 = (bf16[192,4992]{1,0:T(8,128)(2,1)}, bf16[192,4992]{1,0:T(8,128)(2,1)}, u32[]{:S(2)}, u32[]{:S(2)}) collective-permute-start(bf16[192,4992]{1,0:T(8,128)(2,1)} %get-tuple-element.37), channel_id=1, source_target_pairs={{0,4},{2,6},{4,0},{6,2},{1,5},{3,7},{5,1},{7,3}} | collective-permute-start | bytes 5750792 | tf_op jit(solution)/shard_map/ppermute | solution.py:519
  148.5 214.9 %collective-permute-start.2 = (bf16[192,4992]{1,0:T(8,128)(2,1)}, bf16[192,4992]{1,0:T(8,128)(2,1)}, u32[]{:S(2)}, u32[]{:S(2)}) collective-permute-start(bf16[192,4992]{1,0:T(8,128)(2,1)} %get-tuple-element.36), channel_id=1, source_target_pairs={{0,6},{2,4},{4,2},{6,0},{1,7},{3,5},{5,3},{7,1}} | collective-permute-start | bytes 5750792 | tf_op jit(solution)/shard_map/ppermute | solution.py:519
  243.7 108.0 %collective-permute-start.8 = (bf16[192,1536]{1,0:T(8,128)(2,1)}, bf16[192,1536]{1,0:T(8,128)(2,1)S(1)}, u32[]{:S(2)}, u32[]{:S(2)}) collective-permute-start(bf16[192,1536]{1,0:T(8,128)(2,1)} %collective-permute-done.7), channel_id=1, source_target_pairs={{7,5},{0,2}} | collective-permute-start | bytes 1769480 | tf_op jit(solution)/shard_map/ppermute | solution.py:564
  257.6 125.3 %collective-permute-start.14 = (bf16[1120,1536]{1,0:T(8,128)(2,1)}, bf16[1120,1536]{1,0:T(8,128)(2,1)}, u32[]{:S(2)}, u32[]{:S(2)}) collective-permute-start(bf16[1120,1536]{1,0:T(8,128)(2,1)} %get-tuple-element.29), channel_id=1, source_target_pairs={{0,1},{1,0},{2,3},{3,2},{4,5},{5,4},{6,7},{7,6}} | collective-permute-start | bytes 10321928 | tf_op jit(solution)/shard_map/ppermute | solution.py:568
  362.9 11.0 %collective-permute-start.5 = (bf16[192,4992]{1,0:T(8,128)(2,1)}, bf16[192,4992]{1,0:T(8,128)(2,1)S(1)}, u32[]{:S(2)}, u32[]{:S(2)}) collective-permute-start(bf16[192,4992]{1,0:T(8,128)(2,1)} %collective-permute-done.1.refs_2_), channel_id=1, source_target_pairs={{0,1},{1,0},{2,3},{3,2},{4,5},{5,4},{6,7},{7,6}} | collective-permute-start | bytes 5750792 | tf_op jit(solution)/shard_map/ppermute | solution.py:566
  363.3 12.0 %collective-permute-start.6 = (bf16[192,4992]{1,0:T(8,128)(2,1)}, bf16[192,4992]{1,0:T(8,128)(2,1)S(1)}, u32[]{:S(2)}, u32[]{:S(2)}) collective-permute-start(bf16[192,4992]{1,0:T(8,128)(2,1)} %collective-permute-done.2.refs_3_), channel_id=1, source_target_pairs={{0,1},{1,0},{2,3},{3,2},{4,5},{5,4},{6,7},{7,6}} | collective-permute-start | bytes 5750792 | tf_op jit(solution)/shard_map/ppermute | solution.py:566
  887.0 56.5 %collective-permute-start.18 = (f32[4,151936]{1,0:T(4,128)}, f32[4,151936]{1,0:T(4,128)}, u32[]{:S(2)}, u32[]{:S(2)}) collective-permute-start(f32[4,151936]{1,0:T(4,128)} %slice.166), channel_id=1, source_target_pairs={{0,1},{1,0},{2,3},{3,2},{4,5},{5,4},{6,7},{7,6}} | collective-permute-start | bytes 7292936 | tf_op jit(solution)/shard_map/ppermute | solution.py:552
  890.0 61.9 %collective-permute-start.17 = (bf16[2,2048,128]{2,1,0:T(8,128)(2,1)}, bf16[2,2048,128]{2,1,0:T(8,128)(2,1)S(1)}, u32[]{:S(2)}, u32[]{:S(2)}) collective-permute-start(bf16[2,2048,128]{2,1,0:T(8,128)(2,1)} %pad_maximum_fusion.8), channel_id=1, source_target_pairs={{0,6},{2,4},{4,2},{6,0},{1,7},{3,5},{5,3},{7,1}} | collective-permute-start | bytes 3145736 | tf_op jit(solution)/shard_map/ppermute | solution.py:541
  893.0 48.2 %collective-permute-start.16 = (bf16[2,2048,128]{2,1,0:T(8,128)(2,1)}, bf16[2,2048,128]{2,1,0:T(8,128)(2,1)}, u32[]{:S(2)}, u32[]{:S(2)}) collective-permute-start(bf16[2,2048,128]{2,1,0:T(8,128)(2,1)} %pad_maximum_fusion.7), channel_id=1, source_target_pairs={{0,4},{2,6},{4,0},{6,2},{1,5},{3,7},{5,1},{7,3}} | collective-permute-start | bytes 3145736 | tf_op jit(solution)/shard_map/ppermute | solution.py:541
  894.7 44.2 %collective-permute-start.15 = (bf16[2,2048,128]{2,1,0:T(8,128)(2,1)}, bf16[2,2048,128]{2,1,0:T(8,128)(2,1)}, u32[]{:S(2)}, u32[]{:S(2)}) collective-permute-start(bf16[2,2048,128]{2,1,0:T(8,128)(2,1)} %pad_maximum_fusion.6), channel_id=1, source_target_pairs={{0,2},{2,0},{4,6},{6,4},{1,3},{3,1},{5,7},{7,5}} | collective-permute-start | bytes 3145736 | tf_op jit(solution)/shard_map/ppermute | solution.py:541
  948.5 16.6 %collective-permute-start.19 = (f32[1,151936]{1,0:T(1,128)S(1)}, f32[1,151936]{1,0:T(1,128)S(1)}, u32[]{:S(2)}, u32[]{:S(2)}) collective-permute-start(f32[1,151936]{1,0:T(1,128)S(1)} %get-tuple-element.48), channel_id=1, source_target_pairs={{0,2},{2,0},{4,6},{6,4},{1,3},{3,1},{5,7},{7,5}} | collective-permute-start | bytes 1823240 | tf_op jit(solution)/shard_map/ppermute | solution.py:555
  949.5 27.6 %collective-permute-start.20 = (f32[1,151936]{1,0:T(1,128)S(1)}, f32[1,151936]{1,0:T(1,128)S(1)}, u32[]{:S(2)}, u32[]{:S(2)}) collective-permute-start(f32[1,151936]{1,0:T(1,128)S(1)} %get-tuple-element.50), channel_id=1, source_target_pairs={{0,4},{2,6},{4,0},{6,2},{1,5},{3,7},{5,1},{7,3}} | collective-permute-start | bytes 1823240 | tf_op jit(solution)/shard_map/ppermute | solution.py:555
  950.5 26.6 %collective-permute-start.21 = (f32[1,151936]{1,0:T(1,128)S(1)}, f32[1,151936]{1,0:T(1,128)S(1)}, u32[]{:S(2)}, u32[]{:S(2)}) collective-permute-start(f32[1,151936]{1,0:T(1,128)S(1)} %get-tuple-element.49), channel_id=1, source_target_pairs={{0,6},{2,4},{4,2},{6,0},{1,7},{3,5},{5,3},{7,1}} | collective-permute-start | bytes 1823240 | tf_op jit(solution)/shard_map/ppermute | solution.py:555
  (28 other events, 921.4 us)
Sparse Core Ops, SparseCore 0:
  13.8 66.8 all-gather.11
  82.5 95.3 all-gather.7
  179.6 164.5 all-gather.9
  345.9 133.5 all-gather.13
  481.1 129.6 all-gather.15
